TPU v7x, 32 devices: a whole 2x2x4 slice. The times are simulated.
32 devices in a mesh: blk: 8 (over z, y), col: 4 (over x, core).
Axes of the slice: x: 2, y: 2, z: 4, core: 2. Of those that a mesh axis runs over, the one named last changes fastest.
Arguments:
- rank_in: float32 [1024, 512], P(('blk', 'col')), may hold values from 0.5 to 1.5
- delta_in: float32 [1024, 512], P(('blk', 'col'))
- out_degree: int32 [1024, 512], P(('blk', 'col')), may hold values from 26 to 50
- tile_weight: bfloat16 [256, 512, 512], P(('blk', 'col'))
- tile_source: int32 [256], P(('blk', 'col')), may hold values from 0 to 255, as said below
- tile_row: int32 [256], P(('blk', 'col')), may hold values from 0 to 127
- tile_valid: int32 [256], P(('blk', 'col')), may hold values 0 or 1
Outputs:
- rank_out: float32 [1024, 512], P(('blk', 'col'))
- delta_out: float32 [1024, 512], P(('blk', 'col'))
- masses: float32 [6], replicated
Inputs may be any that keep to these rules, and one draw needn't show every extreme that they name: `tile_source`: slot j of the 8 slots of each device (tiles i with i % 8 = j) names a source block from 32 * j to 32 * j + 31.
All inputs are finite; a program needn't handle non-finite values. No bound on the sum of `tile_valid` on one device may be relied on, other than what follows from the above.
Results may differ from a plain program's by a relative error of at most 0.00039.
Values may be sent and summed in bfloat16 or wider, within the bound.
A program may use at most 64 MiB of HBM per device.

v0:
```python
import functools

import jax
import jax.numpy as jnp
from jax import lax
from jax.experimental import pallas as pl
from jax.experimental.pallas import tpu as pltpu
from jax.sharding import PartitionSpec as P

ITERS = 6
damping = 0.85
MESH = pl.DeviceIdType.MESH
F32 = jnp.float32
BF16 = jnp.bfloat16


def exact_pick(onehot, values):
    high = values.astype(BF16)
    rest = values - high.astype(F32)
    middle = rest.astype(BF16)
    low = (rest - middle.astype(F32)).astype(BF16)
    return (
        jnp.dot(onehot, high, preferred_element_type=F32)
        + jnp.dot(onehot, middle, preferred_element_type=F32)
    ) + jnp.dot(onehot, low, preferred_element_type=F32)


def kernel(
    nb,
    nc,
    rank_hbm,
    delta_hbm,
    degree_hbm,
    weight_hbm,
    source_ref,
    row_ref,
    valid_ref,
    total_hbm,
    out_hbm,
    masses_ref,
    weight,
    total,
    delta,
    degree,
    request,
    requests,
    reply,
    replies,
    pick,
    place,
    x_scale,
    rows_out,
    rows_in,
    prods_out,
    prods_in,
    mass_out,
    mass_in,
    load_sem,
    store_sem,
    req_sem,
    reply_send,
    reply_recv,
    rows_send,
    rows_recv,
    prods_send,
    prods_recv,
    mass_sem,
):
    nd = nb * nc
    b, c = lax.axis_index("blk"), lax.axis_index("col")
    me = b * nc + c
    slots = weight.shape[0]
    owned, width = delta.shape
    lanes = request.shape[1]
    chunks = width // 128

    loads = [
        pltpu.make_async_copy(src, dst, load_sem.at[i])
        for i, (src, dst) in enumerate(
            ((delta_hbm, delta), (degree_hbm, degree), (rank_hbm, total), (weight_hbm, weight))
        )
    ]
    for load in loads:
        load.start()

    def others(send):
        def step(off, carry):
            dst = lax.rem(me + off, nd)
            send(dst, (lax.div(dst, nc), lax.rem(dst, nc)))
            return carry

        lax.fori_loop(1, nd, step, 0)

    def remote(src, dst, send_sem, recv_sem, device):
        pltpu.make_async_remote_copy(
            src_ref=src,
            dst_ref=dst,
            send_sem=send_sem,
            recv_sem=recv_sem,
            device_id=device,
            device_id_type=MESH,
        ).start()

    def await_bytes(ref, sem):
        pltpu.make_async_copy(ref, ref, sem).wait()

    barrier = pltpu.get_barrier_semaphore()
    others(
        lambda dst, device: pl.semaphore_signal(
            barrier, inc=1, device_id=device, device_id_type=MESH
        )
    )

    lane = lax.broadcasted_iota(jnp.int32, (1, lanes), 1)
    rows = [row_ref[t] * valid_ref[t] + (valid_ref[t] - 1) for t in range(slots)]
    note = jnp.zeros((1, lanes), jnp.int32)
    for t in range(slots):
        note = jnp.where(lane == c * slots + t, rows[t], note)
        note = jnp.where(lane == nc * slots + t, source_ref[t] - t * owned, note)
    request[...] = note.astype(F32)

    pl.semaphore_wait(barrier, nd - 1)

    def ask(off, carry):
        group = lax.rem(b + off, nb)
        remote(request, requests.at[me], req_sem.at[0], req_sem.at[1], (group, c))
        return carry

    lax.fori_loop(1, nb, ask, 0)
    pltpu.make_async_copy(request, requests.at[me], req_sem.at[1]).start()

    def tell(off, carry):
        column = lax.rem(c + lax.rem(off, nc - 1) + 1, nc)
        group = lax.rem(b + lax.div(off, nc - 1), nb)
        remote(request, requests.at[me], req_sem.at[0], req_sem.at[2], (group, column))
        return carry

    lax.fori_loop(0, nb * (nc - 1), tell, 0)

    loads[0].wait()
    loads[1].wait()
    loads[2].wait()
    mass_lane = lax.broadcasted_iota(jnp.int32, (1, 128), 1)

    def account(step, now, masses):
        total[...] = total[...] + now
        mass = jnp.sum(jnp.sum(jnp.abs(now), axis=0, keepdims=True), axis=1, keepdims=True)
        return jnp.where(mass_lane == step, mass, masses)

    masses = account(0, delta[...], jnp.zeros((1, 128), F32))

    def offsets(asked):
        every = lax.broadcasted_iota(jnp.int32, asked.shape, 1)
        return jnp.sum(jnp.where(every == nc * slots + b, asked, 0.0), axis=1, keepdims=True)

    await_bytes(requests.at[pl.ds(0, nb)], req_sem.at[1])
    wanted = offsets(jnp.concatenate([requests[j * nc + c] for j in range(nb)], axis=0))

    owned_lane = lax.broadcasted_iota(jnp.int32, (nb, owned), 1).astype(F32)
    gather = jnp.where(wanted == owned_lane, 1.0, 0.0).astype(BF16)
    first = exact_pick(gather, delta[...])
    under = exact_pick(gather, degree[...].astype(F32))
    for j in range(nb):
        reply[j, :, :width] = first[j : j + 1]
        reply[j, :, width:] = under[j : j + 1]

    def answer(off, carry):
        group = lax.rem(b + off, nb)
        remote(reply.at[group], replies.at[b], reply_send, reply_recv.at[b], (group, c))
        return carry

    lax.fori_loop(1, nb, answer, 0)
    pltpu.make_async_copy(reply.at[b], replies.at[b], reply_recv.at[b]).start()

    await_bytes(requests.at[pl.ds(0, nd - nb)], req_sem.at[2])
    offset = offsets(jnp.concatenate([requests[d] for d in range(nd)], axis=0))

    height = pick.shape[1]
    line = lax.broadcasted_iota(jnp.int32, (height, 128), 0)
    want = jnp.concatenate([offset, jnp.full((height - nd, 1), -2.0 * nd * owned, F32)], axis=0)
    want = jnp.broadcast_to(want, (height, 128)) + (lax.rem(line, nc) * owned).astype(F32)
    for t in range(slots):
        hit = jnp.where(want == rows[t].astype(F32), 1.0, 0.0)
        pick[t] = jnp.where(line < nd, hit, jnp.where(line == nd + t, 1.0, 0.0))

    reach = requests[b * nc]
    for k in range(1, nc):
        reach = reach + requests[b * nc + k]
    mine = lax.broadcasted_iota(jnp.int32, (owned, nc * slots), 0) + c * owned
    place[...] = jnp.where(mine.astype(F32) == reach[:, : nc * slots], 1.0, 0.0).astype(BF16)

    def nearest(k):
        edge = jnp.minimum(b, nb - 1 - b)
        inner = b + (k + 1) // 2 * (1 if k % 2 else -1)
        outer = jnp.where(2 * b < nb, k, nb - 1 - k)
        return jnp.where(2 * edge >= k, inner, outer)

    loads[3].wait()

    def multiply(step, masses, begin, last):
        result = jnp.zeros((height, width), F32)
        for k in range(nb):
            if not begin and k == (0 if last else 0):
                masses = account(step, gather_owned(step - 1), masses)
                if last:
                    spread(masses)
            t = nearest(k)
            if begin:
                await_bytes(replies.at[t], reply_recv.at[t])
                x_scale[t] = damping / replies[t, :, width:]
                x = replies[t, :, :width]
            else:
                if k % 2 == 0:
                    for i in range(k, min(k + 2, nb)):
                        u = nearest(i)
                        group = rows_in.at[step - 1, pl.ds(u * nc, nc)]
                        await_bytes(group, rows_recv.at[step - 1, u])
                x = rows_in[step - 1, t * nc]
                for i in range(1, nc):
                    x = x + rows_in[step - 1, t * nc + i]
            left = jnp.concatenate([pick[t]] * chunks, axis=1) * (x * x_scale[t])
            result = result + lax.dot_general(
                left.astype(BF16),
                weight[t],
                (((1,), (1,)), ((), ())),
                preferred_element_type=F32,
            )
        if not last:
            for d in range(nd):
                rows_out[step, d] = result[d : d + 1]
            others(
                lambda dst, device: remote(
                    rows_out.at[step, dst],
                    rows_in.at[step, me],
                    rows_send.at[step],
                    rows_recv.at[step, b],
                    device,
                )
            )
            pltpu.make_async_copy(
                rows_out.at[step, me], rows_in.at[step, me], rows_recv.at[step, b]
            ).start()
        prods_out[step] = result[nd : nd + slots]
        for k in range(1, nc):
            remote(
                prods_out.at[step],
                prods_in.at[step, c],
                prods_send.at[step],
                prods_recv.at[step],
                (b, lax.rem(c + k, nc)),
            )
        pltpu.make_async_copy(
            prods_out.at[step], prods_in.at[step, c], prods_recv.at[step]
        ).start()
        return masses

    def gather_owned(step):
        await_bytes(prods_in.at[step], prods_recv.at[step])
        return exact_pick(place[...], prods_in[step].reshape(nc * slots, width))

    def spread(masses):
        mass_out[...] = masses
        others(
            lambda dst, device: remote(
                mass_out, mass_in.at[me], mass_sem.at[0], mass_sem.at[1], device
            )
        )
        pltpu.make_async_copy(mass_out, mass_in.at[me], mass_sem.at[1]).start()

    masses = multiply(0, masses, True, False)
    masses = lax.fori_loop(
        1, ITERS - 1, lambda step, masses: multiply(step, masses, False, False), masses
    )
    multiply(ITERS - 1, masses, False, True)
    total_store = pltpu.make_async_copy(total, total_hbm, store_sem.at[0])
    total_store.start()
    delta[...] = gather_owned(ITERS - 1)
    out_store = pltpu.make_async_copy(delta, out_hbm, store_sem.at[1])
    out_store.start()

    await_bytes(mass_in, mass_sem.at[1])
    summed = mass_in[0]
    for d in range(1, nd):
        summed = summed + mass_in[d]
    summed = summed / float(nd * owned * width)
    for t in range(ITERS):
        masses_ref[t] = jnp.sum(jnp.where(mass_lane == t, summed, 0.0))

    await_bytes(requests.at[pl.ds(0, nd - 1)], req_sem.at[0])
    await_bytes(replies.at[pl.ds(0, nb - 1)], reply_send)
    await_bytes(mass_in.at[pl.ds(0, nd - 1)], mass_sem.at[0])
    for step in range(ITERS):
        if step < ITERS - 1:
            await_bytes(rows_out.at[step, pl.ds(0, nd - 1)], rows_send.at[step])
        await_bytes(prods_in.at[step, pl.ds(0, nc - 1)], prods_send.at[step])
    total_store.wait()
    out_store.wait()


def on_device(rank_in, delta_in, out_degree, tile_weight, tile_source, tile_row, tile_valid):
    owned, width = delta_in.shape
    slots = tile_weight.shape[0]
    nb = lax.axis_size("blk")
    nc = lax.axis_size("col")
    nd = nb * nc
    lanes = -(-(slots * (nc + 1)) // 128) * 128
    height = -(-(nd + slots) // 16) * 16
    hbm = pl.BlockSpec(memory_space=pl.ANY)
    smem = pl.BlockSpec(memory_space=pltpu.SMEM)
    dma = pltpu.SemaphoreType.DMA
    return pl.pallas_call(
        functools.partial(kernel, nb, nc),
        out_shape=(
            jax.ShapeDtypeStruct((owned, width), F32),
            jax.ShapeDtypeStruct((owned, width), F32),
            jax.ShapeDtypeStruct((ITERS,), F32),
        ),
        in_specs=[hbm] * 4 + [smem] * 3,
        out_specs=(hbm, hbm, smem),
        scratch_shapes=[
            pltpu.VMEM((slots, width, width), BF16),
            pltpu.VMEM((owned, width), F32),
            pltpu.VMEM((owned, width), F32),
            pltpu.VMEM((owned, width), jnp.int32),
            pltpu.VMEM((1, lanes), F32),
            pltpu.VMEM((nd, 1, lanes), F32),
            pltpu.VMEM((nb, 1, 2 * width), F32),
            pltpu.VMEM((nb, 1, 2 * width), F32),
            pltpu.VMEM((slots, height, 128), F32),
            pltpu.VMEM((owned, nc * slots), BF16),
            pltpu.VMEM((nb, 1, width), F32),
            pltpu.VMEM((ITERS - 1, nd, 1, width), F32),
            pltpu.VMEM((ITERS - 1, nd, 1, width), F32),
            pltpu.VMEM((ITERS, slots, width), F32),
            pltpu.VMEM((ITERS, nc, slots, width), F32),
            pltpu.VMEM((1, 128), F32),
            pltpu.VMEM((nd, 1, 128), F32),
            dma((4,)),
            dma((2,)),
            dma((3,)),
            dma,
            dma((nb,)),
            dma((ITERS - 1,)),
            dma((ITERS - 1, nb)),
            dma((ITERS,)),
            dma((ITERS,)),
            dma((2,)),
        ],
        compiler_params=pltpu.CompilerParams(
            collective_id=0, has_side_effects=True, vmem_limit_bytes=60 * 1024 * 1024
        ),
    )(rank_in, delta_in, out_degree, tile_weight, tile_source, tile_row, tile_valid)


def solution(mesh):
    return jax.shard_map(
        on_device,
        mesh=mesh,
        in_specs=(
            P(("blk", "col"), None),
            P(("blk", "col"), None),
            P(("blk", "col"), None),
            P(("blk", "col"), None, None),
            P(("blk", "col")),
            P(("blk", "col")),
            P(("blk", "col")),
        ),
        out_specs=(P(("blk", "col"), None), P(("blk", "col"), None), P()),
        check_vma=False,
    )
```

profile of v0, /device:TPU:0, one launch (start us, length us, event | category | flops | bytes accessed | tf_op | source)
XLA Modules:
  0.0 52.6 jit_solution(2365627380556844659)
XLA Ops:
  0.6 47.9 %shard_map.94 = (f32[32,512]{1,0:T(8,128)}, f32[32,512]{1,0:T(8,128)}, f32[6]{0:T(128)}) custom-call(f32[32,512]{1,0:T(8,128)} %rank_hbm.1, f32[32,512]{1,0:T(8,128)} %delta_hbm.1, s32[32,512]{1,0:T(8,128)} %degree_hbm.1, bf16[8,512,512]{2,1,0:T(8,128)(2,1)} %weight_hbm.1, s32[8]{0:T(128)} %source_ref.1, s32[8]{0:T(128)} %row_ref.1, s32[8]{0:T(128)} %valid_ref.1), custom_call_target="tpu_custom_call" | custom-call | tf_op jit(solution)/shard_map/pallas_call | solution.py:311
  48.5 1.5 %copy.13 = f32[32,512]{1,0:T(8,128)} copy(f32[32,512]{1,0:T(8,128)} %get-tuple-element.6) | data formatting | bytes 131072
  50.0 1.5 %copy.14 = f32[32,512]{1,0:T(8,128)} copy(f32[32,512]{1,0:T(8,128)} %get-tuple-element.7) | data formatting | bytes 131072
  51.4 1.2 %copy.15 = f32[6]{0:T(128)} copy(f32[6]{0:T(128)} %get-tuple-element.8) | data formatting | bytes 48
where the time goes:
time: 52.9 us; the launch traced here: 52.6 us
  Pallas kernels  47.9 us (91%)
  local copies, waits for them, and re-layouts  4.12 us (8%)
  between operations  0.64 us (1%)
    pallas_call x1, Pallas kernels, on_device(): pl.pallas_call(functools.partial(kernel, nb, nc), out_shape=(jax.ShapeDty...  47.9 us
    unnamed x3, local copies, waits for them, and re-layouts  4.12 us

commit v1 on v0

--- a/solution.py
+++ b/solution.py
@@ -35,12 +35,10 @@
     source_ref,
     row_ref,
     valid_ref,
-    total_hbm,
-    out_hbm,
+    total,
+    delta,
     masses_ref,
     weight,
-    total,
-    delta,
     degree,
     request,
     requests,
@@ -56,7 +54,6 @@
     mass_out,
     mass_in,
     load_sem,
-    store_sem,
     req_sem,
     reply_send,
     reply_recv,
@@ -228,15 +225,17 @@
         if not last:
             for d in range(nd):
                 rows_out[step, d] = result[d : d + 1]
-            others(
-                lambda dst, device: remote(
-                    rows_out.at[step, dst],
-                    rows_in.at[step, me],
-                    rows_send.at[step],
-                    rows_recv.at[step, b],
-                    device,
-                )
-            )
+            for k in reversed(range(nb)):
+                g = nearest(k)
+                for i in range(1 if k == 0 else 0, nc):
+                    e = lax.rem(c + i, nc)
+                    remote(
+                        rows_out.at[step, g * nc + e],
+                        rows_in.at[step, me],
+                        rows_send.at[step],
+                        rows_recv.at[step, b],
+                        (g, e),
+                    )
             pltpu.make_async_copy(
                 rows_out.at[step, me], rows_in.at[step, me], rows_recv.at[step, b]
             ).start()
@@ -272,19 +271,14 @@
         1, ITERS - 1, lambda step, masses: multiply(step, masses, False, False), masses
     )
     multiply(ITERS - 1, masses, False, True)
-    total_store = pltpu.make_async_copy(total, total_hbm, store_sem.at[0])
-    total_store.start()
     delta[...] = gather_owned(ITERS - 1)
-    out_store = pltpu.make_async_copy(delta, out_hbm, store_sem.at[1])
-    out_store.start()
 
     await_bytes(mass_in, mass_sem.at[1])
     summed = mass_in[0]
     for d in range(1, nd):
         summed = summed + mass_in[d]
     summed = summed / float(nd * owned * width)
-    for t in range(ITERS):
-        masses_ref[t] = jnp.sum(jnp.where(mass_lane == t, summed, 0.0))
+    masses_ref[...] = summed
 
     await_bytes(requests.at[pl.ds(0, nd - 1)], req_sem.at[0])
     await_bytes(replies.at[pl.ds(0, nb - 1)], reply_send)
@@ -293,8 +287,22 @@
         if step < ITERS - 1:
             await_bytes(rows_out.at[step, pl.ds(0, nd - 1)], rows_send.at[step])
         await_bytes(prods_in.at[step, pl.ds(0, nc - 1)], prods_send.at[step])
-    total_store.wait()
-    out_store.wait()
+
+
+def finish(total, delta, masses, total_hbm, out_hbm, masses_hbm, mass, sem):
+    stores = [
+        pltpu.make_async_copy(total, total_hbm, sem.at[0]),
+        pltpu.make_async_copy(delta, out_hbm, sem.at[1]),
+        pltpu.make_async_copy(mass, masses_hbm, sem.at[2]),
+    ]
+    stores[0].start()
+    stores[1].start()
+    lane = lax.broadcasted_iota(jnp.int32, (1, 128), 1)
+    for t in range(ITERS):
+        mass[t] = jnp.sum(jnp.where(lane == t, masses[...], 0.0))
+    stores[2].start()
+    for store in stores:
+        store.wait()
 
 
 def on_device(rank_in, delta_in, out_degree, tile_weight, tile_source, tile_row, tile_valid):
@@ -307,20 +315,19 @@
     height = -(-(nd + slots) // 16) * 16
     hbm = pl.BlockSpec(memory_space=pl.ANY)
     smem = pl.BlockSpec(memory_space=pltpu.SMEM)
+    vmem = pl.BlockSpec(memory_space=pltpu.VMEM)
     dma = pltpu.SemaphoreType.DMA
-    return pl.pallas_call(
+    total, delta, masses = pl.pallas_call(
         functools.partial(kernel, nb, nc),
         out_shape=(
-            jax.ShapeDtypeStruct((owned, width), F32),
-            jax.ShapeDtypeStruct((owned, width), F32),
-            jax.ShapeDtypeStruct((ITERS,), F32),
+            pltpu.VMEM((owned, width), F32),
+            pltpu.VMEM((owned, width), F32),
+            pltpu.VMEM((1, 128), F32),
         ),
         in_specs=[hbm] * 4 + [smem] * 3,
-        out_specs=(hbm, hbm, smem),
+        out_specs=(vmem, vmem, vmem),
         scratch_shapes=[
             pltpu.VMEM((slots, width, width), BF16),
-            pltpu.VMEM((owned, width), F32),
-            pltpu.VMEM((owned, width), F32),
             pltpu.VMEM((owned, width), jnp.int32),
             pltpu.VMEM((1, lanes), F32),
             pltpu.VMEM((nd, 1, lanes), F32),
@@ -336,7 +343,6 @@
             pltpu.VMEM((1, 128), F32),
             pltpu.VMEM((nd, 1, 128), F32),
             dma((4,)),
-            dma((2,)),
             dma((3,)),
             dma,
             dma((nb,)),
@@ -350,6 +356,18 @@
             collective_id=0, has_side_effects=True, vmem_limit_bytes=60 * 1024 * 1024
         ),
     )(rank_in, delta_in, out_degree, tile_weight, tile_source, tile_row, tile_valid)
+    return pl.pallas_call(
+        finish,
+        out_shape=(
+            jax.ShapeDtypeStruct((owned, width), F32),
+            jax.ShapeDtypeStruct((owned, width), F32),
+            jax.ShapeDtypeStruct((ITERS,), F32),
+        ),
+        in_specs=[vmem] * 3,
+        out_specs=(hbm, hbm, hbm),
+        scratch_shapes=[pltpu.SMEM((ITERS,), F32), dma((3,))],
+        compiler_params=pltpu.CompilerParams(vmem_limit_bytes=4 * 1024 * 1024),
+    )(total, delta, masses)
 
 
 def solution(mesh):

time: 52.9 us -> 47.3 us (0.89)
  local copies, waits for them, and re-layouts: 4.12 us -> 0 us
  Pallas kernels: 47.9 us -> 46.4 us
    unnamed x3 -> x0, local copies, waits for them, and re-layouts: 4.12 us -> none
    pallas_call x1 -> x2, Pallas kernels: 47.9 us -> 46.4 us  [the longest x1 45.8 us: on_device(): pl.pallas_call(functools.partial(kernel, nb, nc), out_shape=(pltpu.VMEM((...]
where the time goes in v1:
time: 47.3 us; the launch traced here: 47.1 us
  Pallas kernels  46.4 us (98%)
  between operations  0.64 us (1%)
    pallas_call x1, Pallas kernels, on_device(): pl.pallas_call(functools.partial(kernel, nb, nc), out_shape=(pltpu.VMEM((...  45.8 us

profile of v1, /device:TPU:0, one launch (start us, length us, event | category | flops | bytes accessed | tf_op | source)
XLA Modules:
  0.0 47.1 jit_solution(656257682686742192)
XLA Ops:
  0.6 45.8 %shard_map.94 = (f32[32,512]{1,0:T(8,128)S(1)}, f32[32,512]{1,0:T(8,128)S(1)}, f32[1,128]{1,0:T(1,128)S(1)}) custom-call(f32[32,512]{1,0:T(8,128)} %rank_hbm.1, f32[32,512]{1,0:T(8,128)} %delta_hbm.1, s32[32,512]{1,0:T(8,128)} %degree_hbm.1, bf16[8,512,512]{2,1,0:T(8,128)(2,1)} %weight_hbm.1, s32[8]{0:T(128)} %source_ref.1, s32[8]{0:T(128)} %row_ref.1, ...), custom_call_target="tpu_custom_call" | custom-call | tf_op jit(solution)/shard_map/pallas_call | solution.py:320
  46.4 0.7 %shard_map.95 = (f32[32,512]{1,0:T(8,128)}, f32[32,512]{1,0:T(8,128)}, f32[6]{0:T(128)}) custom-call(f32[32,512]{1,0:T(8,128)S(1)} %get-tuple-element.6.total, f32[32,512]{1,0:T(8,128)S(1)} %get-tuple-element.7.delta, f32[1,128]{1,0:T(1,128)S(1)} %get-tuple-element.8.masses), custom_call_target="tpu_custom_call" | custom-call | tf_op jit(solution)/shard_map/pallas_call | solution.py:359
